TPU v7x, 32 devices: a whole 2x2x4 slice. The times are simulated.
32 devices in a mesh: enc: 8 (over z, x), section: 2 (over core), llmdp: 2 (over y).
Axes of the slice: x: 2, y: 2, z: 4, core: 2. Of those that a mesh axis runs over, the one named last changes fastest.
Arguments:
- patches: bfloat16 [2048, 3200], P('enc', ('section', 'llmdp')), may hold values from -6 to 6
- gain: float32 [3200], replicated, may hold values from 0.25 to 1.75
- shift: float32 [3200], replicated, may hold values from -3 to 3
- proj_weight: bfloat16 [3200, 8192], P('enc', ('section', 'llmdp')), may hold values from -0.109375 to 0.109375
- llm_rank: int32 [2048, 1], P('enc'), may hold values from 0 to 7; in each aligned block of 256 rows (0 to 255, 256 to 511, ...) at most 96 rows name the same one
- embed_grad: bfloat16 [6144, 8192], P('enc', ('section', 'llmdp')), may hold values from -0.59765625 to 0.59765625
Outputs:
- embeds_recv: bfloat16 [6144, 8192], P('enc', ('section', 'llmdp'))
- hidden_state_gradient: bfloat16 [2048, 3200], P('enc', ('section', 'llmdp'))
- grad_weight: float32 [3200, 8192], P('enc', ('section', 'llmdp'))
- gain_gradient: float32 [3200], P(('section', 'llmdp'))
- grad_shift: float32 [3200], P(('section', 'llmdp'))
Inputs may be any that keep to these rules, and one draw needn't show every extreme that they name: `llm_rank`: among the 256 rows of one device, at most 96 name the same owner, a bound that some block reaches.
All inputs are finite; a program needn't handle non-finite values.
Results may differ from a plain program's by a relative error of at most 0.018.
Values may be sent and summed in bfloat16 or wider, within the bound.
A program may use at most 128 MiB of HBM per device.

v0:
```python
import jax
import jax.numpy as jnp
from jax import lax
from jax.sharding import PartitionSpec as P

EPSILON = 1e-05
MAX_BLOCK = 2


def block_size(senders, out_cols):
    size = MAX_BLOCK
    while size > 1 and (senders % size or senders == size or out_cols % (size * 128)):
        size //= 2
    return size


def body(patches, gain, shift, proj_weight, llm_rank, embed_grad):
    features = ("section", "llmdp")
    own_rows, owned_width = patches.shape
    width = gain.shape[0]
    weight_rows, out_cols = proj_weight.shape
    senders = lax.axis_size("enc")
    block = block_size(senders, out_cols)
    near = [[b * block + i for i in range(block)] for b in range(senders // block)]
    far = [[b * block + i for b in range(senders // block)] for i in range(block)]

    def near_exchange(x, split, concat):
        return lax.all_to_all(x, "enc", split, concat, axis_index_groups=near, tiled=True)

    column_start = lax.axis_index(features) * owned_width
    gain_own = lax.dynamic_slice_in_dim(gain, column_start, owned_width, 0)
    weight_part = near_exchange(proj_weight, 1, 0)
    weight = lax.all_gather(weight_part, "enc", axis=0, axis_index_groups=far, tiled=True)
    block_rows = lax.all_gather(patches, "enc", axis=0, axis_index_groups=near, tiled=True)
    complete_rows = lax.all_gather(block_rows, features, axis=1, tiled=True).astype(jnp.float32)
    row_average = jnp.mean(complete_rows, 1, keepdims=True)
    variance = jnp.mean(complete_rows * complete_rows, 1, keepdims=True) - row_average * row_average
    inverse_deviation = lax.rsqrt(variance + EPSILON)
    standardized = (complete_rows - row_average) * inverse_deviation
    normed = (standardized * gain + shift).astype(jnp.bfloat16)
    row_start = lax.axis_index("enc") % block * own_rows
    average_own = lax.dynamic_slice_in_dim(row_average, row_start, own_rows, 0)
    deviation_own = lax.dynamic_slice_in_dim(inverse_deviation, row_start, own_rows, 0)
    standardized_owned = (patches.astype(jnp.float32) - average_own) * deviation_own
    most_slots = embed_grad.shape[0] // senders
    target = llm_rank[:, 0]
    owners = jnp.arange(senders, dtype=jnp.int32)
    hits = (target[:, None] == owners[None, :]).astype(jnp.int32)
    rank = jnp.sum((jnp.cumsum(hits, 0) - hits) * hits, 1)
    slot = target * most_slots + rank

    def enc_exchange(x):
        return lax.all_to_all(
            x.reshape(senders, most_slots, out_cols), "enc", split_axis=0, concat_axis=0, tiled=True
        ).reshape(senders * most_slots, out_cols)

    d_embed = near_exchange(enc_exchange(embed_grad)[slot], 1, 0)
    grad_part = lax.psum_scatter(
        lax.dot_general(
            normed, d_embed, (((0,), (0,)), ((), ())), preferred_element_type=jnp.float32
        ).astype(jnp.bfloat16),
        "enc",
        scatter_dimension=0,
        axis_index_groups=far,
        tiled=True,
    )
    grad_weight = near_exchange(grad_part, 0, 1).astype(jnp.float32)
    embed_part = jnp.dot(normed, weight, preferred_element_type=jnp.float32).astype(jnp.bfloat16)
    embed = near_exchange(embed_part, 0, 1)
    outgoing = jnp.zeros((senders * most_slots, out_cols), jnp.bfloat16).at[slot].set(embed)
    embeds_recv = enc_exchange(outgoing)
    partial_grad = lax.dot_general(
        d_embed, weight, (((1,), (1,)), ((), ())), preferred_element_type=jnp.float32
    )
    group_count = width // owned_width
    pieces = partial_grad.astype(jnp.bfloat16).reshape(block * own_rows, group_count, owned_width)
    columns = lax.all_to_all(pieces, features, split_axis=1, concat_axis=1, tiled=True)
    column_sum = jnp.sum(columns.astype(jnp.float32), 1).astype(jnp.bfloat16)
    shares = near_exchange(column_sum.reshape(block, own_rows, owned_width), 0, 0)
    owned_normalized_gradient = jnp.sum(shares.astype(jnp.float32), 0)
    owned_centered_gradient = owned_normalized_gradient * gain_own
    mean_sum, cross_sum = lax.psum(
        (
            jnp.sum(owned_centered_gradient, 1),
            jnp.sum(owned_centered_gradient * standardized_owned, 1),
        ),
        features,
    )
    gradient_row_average = (mean_sum / width)[:, None]
    gradient_cross_product = (cross_sum / width)[:, None]
    hidden_state_gradient = (
        deviation_own
        * (
            owned_centered_gradient
            - gradient_row_average
            - standardized_owned * gradient_cross_product
        )
    ).astype(jnp.bfloat16)
    gain_gradient, grad_shift = lax.psum(
        (
            jnp.sum(owned_normalized_gradient * standardized_owned, 0),
            jnp.sum(owned_normalized_gradient, 0),
        ),
        "enc",
    )
    return (embeds_recv, hidden_state_gradient, grad_weight, gain_gradient, grad_shift)


def solution(mesh):
    in_specs = (
        P("enc", ("section", "llmdp")),
        P(),
        P(),
        P("enc", ("section", "llmdp")),
        P("enc", None),
        P("enc", ("section", "llmdp")),
    )
    out_specs = (
        P("enc", ("section", "llmdp")),
        P("enc", ("section", "llmdp")),
        P("enc", ("section", "llmdp")),
        P(("section", "llmdp")),
        P(("section", "llmdp")),
    )
    return jax.shard_map(body, mesh=mesh, in_specs=in_specs, out_specs=out_specs, check_vma=False)
```

profile of v0, /device:TPU:0, one launch (start us, length us, event | category | flops | bytes accessed | tf_op | source)
XLA Modules:
  0.0 466.7 jit_solution(16512288865410212296)
XLA Ops:
  7.2 0.0 all-gather.3.cloned.1.call-start
  7.2 15.1 %all_gather.9 = bf16[512,800]{0,1:T(8,128)(2,1)} all-gather(bf16[256,800]{0,1:T(8,128)(2,1)} %param.6), channel_id=1, replica_groups={{0,4},{8,12},{16,20},{24,28},{1,5},{9,13},{17,21},{25,29},{2,6},{10,14}..., dimensions={0}, use_global_device_ids=true | all-gather | bytes 1228800 | tf_op jit(solution)/shard_map/all_gather | solution.py:34
  22.4 0.0 all-gather.5.cloned.1.call-start
  22.4 1.6 copy.36
  24.0 23.0 %all_to_all.90 = bf16[400,2,1024]{2,0,1:T(8,128)(2,1)} all-to-all(bf16[400,2,1024]{2,0,1:T(8,128)(2,1)S(1)} %bitcast.54), channel_id=1, replica_groups={{0,4},{8,12},{16,20},{24,28},{1,5},{9,13},{17,21},{25,29},{2,6},{10,14}..., dimensions={1} | all-to-all | bytes 3276800 | tf_op jit(solution)/shard_map/all_to_all | solution.py:28
  47.0 4.9 %all-to-all-start.3 = ((bf16[8,96,2048]{2,1,0:T(8,128)(2,1)}), bf16[8,96,2048]{2,1,0:T(8,128)(2,1)S(1)}, u32[]{:S(2)}, u32[]{:S(2)}) async-start(bf16[8,96,2048]{2,1,0:T(8,128)(2,1)} %bitcast.58), calls=%async_computation.3 | async-start | bytes 6291456 | tf_op jit(solution)/shard_map/all_to_all | solution.py:53
  51.9 0.6 reduce-window.6
  52.5 0.2 slice_reduce_fusion
  52.8 0.1 fusion.8
  52.9 139.4 %all-to-all-done.3 = bf16[8,96,2048]{2,1,0:T(8,128)(2,1)S(1)} async-done(((bf16[8,96,2048]{2,1,0:T(8,128)(2,1)}), bf16[8,96,2048]{2,1,0:T(8,128)(2,1)S(1)}, u32[]{:S(2)}, u32[]{:S(2)}) %all-to-all-start.3) | async-done | bytes 3145760 | tf_op jit(solution)/shard_map/all_to_all | solution.py:53
  192.3 2.3 gather_fusion
  194.6 2.3 copy.37
  196.9 9.7 %all-to-all-start.4 = ((bf16[256,2,1024]{2,0,1:T(8,128)(2,1)}), bf16[256,2,1024]{2,0,1:T(8,128)(2,1)}, u32[]{:S(2)}, u32[]{:S(2)}) async-start(bf16[256,2,1024]{2,0,1:T(8,128)(2,1)} %bitcast.46), calls=%async_computation.4 | async-start | bytes 2097152 | tf_op jit(solution)/shard_map/all_to_all | solution.py:28
  206.6 3.0 convert_reduce_fusion
  209.6 7.6 %all-to-all-done.4 = bf16[256,2,1024]{2,0,1:T(8,128)(2,1)} async-done(((bf16[256,2,1024]{2,0,1:T(8,128)(2,1)}), bf16[256,2,1024]{2,0,1:T(8,128)(2,1)}, u32[]{:S(2)}, u32[]{:S(2)}) %all-to-all-start.4) | async-done | bytes 1048608 | tf_op jit(solution)/shard_map/all_to_all | solution.py:28
  217.2 7.5 %convolution_convert_fusion = bf16[3200,1024]{1,0:T(8,128)(2,1)} fusion(bf16[512,1024]{1,0:T(8,128)(2,1)} %bitcast.16, bf16[512,3200]{0,1:T(8,128)(2,1)S(1)} %copy-done.2, f32[3200]{0:T(1024)S(1)} %copy-done.8, f32[3200]{0:T(1024)S(1)} %copy-done.7, f32[512]{0:T(512)S(1)} %get-tuple-element.17, f32[512]{0:T(512)S(1)} %get-tuple-element.16), kind=kOutput, calls=%fused_computation.5 | convolution fusion | flops 3368550400 | bytes 10908672 | tf_op jit(solution)/shard_map/dot_general | solution.py:59
  224.8 2.2 all-gather.5.cloned.1.call-done
  227.0 6.9 %convolution_convert_fusion.1 = bf16[512,3200]{1,0:T(8,128)(2,1)S(1)} fusion(bf16[512,1024]{1,0:T(8,128)(2,1)} %bitcast.16, bf16[3200,1024]{1,0:T(8,128)(2,1)} %all-gather.5.cloned.1.call-done), kind=kOutput, calls=%fused_computation.11 | convolution fusion | flops 3357081600 | bytes 10878976 | tf_op jit(solution)/shard_map/dot_general | solution.py:72
  233.9 3.4 copy.26
  237.4 3.9 all-to-all-start.5
  241.3 8.7 %convolution_convert_fusion.2 = bf16[512,1024]{1,0:T(8,128)(2,1)} fusion(bf16[3200,1024]{1,0:T(8,128)(2,1)} %all-gather.5.cloned.1.call-done, bf16[512,3200]{0,1:T(8,128)(2,1)} %all-gather.3.cloned.1.call-done, f32[3200]{0:T(1024)S(1)} %copy-done.8, f32[3200]{0:T(1024)S(1)} %copy-done.7, f32[512]{0:T(512)S(1)} %get-tuple-element.17, ...), kind=kOutput, calls=%fused_computation.18 | convolution fusion | flops 3365797888 | bytes 10908672 | tf_op jit(solution)/shard_map/dot_general | solution.py:68
  250.0 2.3 copy.23
  252.3 27.1 %all-to-all-done.5 = bf16[512,4,800]{0,2,1:T(8,128)(2,1)S(1)} async-done(((bf16[512,4,800]{0,2,1:T(8,128)(2,1)}), bf16[512,4,800]{0,2,1:T(8,128)(2,1)S(1)}, u32[]{:S(2)}, u32[]{:S(2)}) %all-to-all-start.5) | async-done | bytes 3276832 | tf_op jit(solution)/shard_map/all_to_all | solution.py:77
  279.4 4.4 all-to-all-start.1
  283.8 1.6 reduce_sum.90
  285.4 2.1 copy.38
  287.5 10.1 %all-to-all-done.1 = bf16[2,256,1024]{1,2,0:T(8,128)(2,1)} async-done(((bf16[2,256,1024]{1,2,0:T(8,128)(2,1)}), bf16[2,256,1024]{1,2,0:T(8,128)(2,1)}, u32[]{:S(2)}, u32[]{:S(2)}) %all-to-all-start.1) | async-done | bytes 1048608 | tf_op jit(solution)/shard_map/all_to_all | solution.py:28
  297.6 3.5 all-to-all-start.6
  301.1 1.5 copy.24
  302.6 4.3 scatter_custom_fusion
  306.9 4.6 all-to-all-done.6
  311.5 0.9 copy-done.3
  312.4 9.3 %all-to-all-start.2 = ((bf16[8,96,2048]{2,1,0:T(8,128)(2,1)}), bf16[8,96,2048]{2,1,0:T(8,128)(2,1)S(1)}, u32[]{:S(2)}, u32[]{:S(2)}) async-start(bf16[8,96,2048]{2,1,0:T(8,128)(2,1)} %bitcast.52), calls=%async_computation.2 | async-start | bytes 6291456 | tf_op jit(solution)/shard_map/all_to_all | solution.py:53
  321.7 1.4 dynamic_slice.8
  323.1 1.3 dynamic-slice.3
  324.4 1.3 dynamic-slice.4
  325.8 87.7 %all-to-all-done.2 = bf16[8,96,2048]{2,1,0:T(8,128)(2,1)S(1)} async-done(((bf16[8,96,2048]{2,1,0:T(8,128)(2,1)}), bf16[8,96,2048]{2,1,0:T(8,128)(2,1)S(1)}, u32[]{:S(2)}, u32[]{:S(2)}) %all-to-all-start.2) | async-done | bytes 3145760 | tf_op jit(solution)/shard_map/all_to_all | solution.py:53
  413.5 4.6 all-to-all-start.7
  418.2 2.0 convert_reduce_fusion.1
  420.2 0.9 copy-done
  421.1 1.7 multiply_reduce_fusion
  422.8 8.2 %all-reduce.1 = (f32[256]{0:T(256)}, f32[256]{0:T(256)}) all-reduce(f32[256]{0:T(256)} %get-tuple-element.8, f32[256]{0:T(256)} %get-tuple-element.9), channel_id=1, replica_groups=mesh['enc'=8,'section'=2,'llmdp'=2] {'section','llmdp'}, use_global_device_ids=true, to_apply=%region_11.12 | all-reduce | flops 512 | bytes 4096 | tf_op jit(solution)/shard_map/psum | solution.py:82
  431.0 20.9 %all-reduce = (f32[800]{0:T(1024)}, f32[800]{0:T(1024)}) all-reduce(f32[800]{0:T(1024)} %get-tuple-element.7, f32[800]{0:T(1024)} %get-tuple-element.10), channel_id=1, replica_groups=mesh['enc'=8,'section'=2,'llmdp'=2] {'enc'}, use_global_device_ids=true, to_apply=%region_14.15 | all-reduce | flops 1600 | bytes 12800 | tf_op jit(solution)/shard_map/psum | solution.py:99
  451.9 0.7 broadcast_multiply_fusion.1
  452.6 2.1 multiply_convert_fusion
  454.7 1.8 convert_bitcast_fusion
  456.5 1.9 copy.32
  458.5 1.7 copy.40
  (29 shorter events, 0.2 us)
Async XLA Ops:
  7.2 199.4 %all-gather.3.cloned.1.call-start = ((), (), s32[]{:S(2)}) async-start(), calls=%async_computation.9 | async-start | bytes 4096000 | tf_op jit(solution)/shard_map/all_gather | solution.py:35
  22.4 204.6 %all-gather.5.cloned.1.call-start = ((), (), s32[]{:S(2)}) async-start(), calls=%async_computation.10 | async-start | bytes 8192000 | tf_op jit(solution)/shard_map/all_gather | solution.py:33
  47.0 4.9 %copy-start.4 = (s32[256,1]{0,1:T(1,128)S(1)}, s32[256,1]{0,1:T(1,128)}, u32[]{:S(2)}) copy-start(s32[256,1]{0,1:T(1,128)} %param.10) | copy-start | bytes 3076
  47.0 145.3 %all-to-all-start.3 = ((bf16[8,96,2048]{2,1,0:T(8,128)(2,1)}), bf16[8,96,2048]{2,1,0:T(8,128)(2,1)S(1)}, u32[]{:S(2)}, u32[]{:S(2)}) async-start(bf16[8,96,2048]{2,1,0:T(8,128)(2,1)} %bitcast.58), calls=%async_computation.3 | async-start | bytes 6291456 | tf_op jit(solution)/shard_map/all_to_all | solution.py:53
  194.6 22.6 %copy-start.7 = (f32[3200]{0:T(1024)S(1)}, f32[3200]{0:T(1024)}, u32[]{:S(2)}) copy-start(f32[3200]{0:T(1024)} %param.7) | copy-start | bytes 38404
  194.6 22.6 %copy-start.8 = (f32[3200]{0:T(1024)S(1)}, f32[3200]{0:T(1024)}, u32[]{:S(2)}) copy-start(f32[3200]{0:T(1024)} %param.8) | copy-start | bytes 38404
  196.9 20.3 %all-to-all-start.4 = ((bf16[256,2,1024]{2,0,1:T(8,128)(2,1)}), bf16[256,2,1024]{2,0,1:T(8,128)(2,1)}, u32[]{:S(2)}, u32[]{:S(2)}) async-start(bf16[256,2,1024]{2,0,1:T(8,128)(2,1)} %bitcast.46), calls=%async_computation.4 | async-start | bytes 2097152 | tf_op jit(solution)/shard_map/all_to_all | solution.py:28
  206.6 206.9 %reduce-scatter.2.cloned.1.call-start = ((), (), s32[]{:S(2)}) async-start(), calls=%async_computation.11 | async-start | bytes 8192000 | tf_op jit(solution)/shard_map/reduce_scatter | solution.py:58
  206.6 10.6 %copy-start.2 = (bf16[512,3200]{0,1:T(8,128)(2,1)S(1)}, bf16[512,3200]{0,1:T(8,128)(2,1)}, u32[]{:S(2)}) copy-start(bf16[512,3200]{0,1:T(8,128)(2,1)} %all-gather.3.cloned.1.call-done) | copy-start | bytes 9830404
  209.6 31.7 %copy-start.5 = (f32[512]{0:T(512)}, f32[512]{0:T(512)S(1)}, u32[]{:S(2)}) copy-start(f32[512]{0:T(512)S(1)} %get-tuple-element.17) | copy-start | bytes 6148
  209.6 31.7 %copy-start.6 = (f32[512]{0:T(512)}, f32[512]{0:T(512)S(1)}, u32[]{:S(2)}) copy-start(f32[512]{0:T(512)S(1)} %get-tuple-element.16) | copy-start | bytes 6148
  237.4 42.0 %all-to-all-start.5 = ((bf16[512,4,800]{0,2,1:T(8,128)(2,1)}), bf16[512,4,800]{0,2,1:T(8,128)(2,1)S(1)}, u32[]{:S(2)}, u32[]{:S(2)}) async-start(bf16[512,4,800]{0,2,1:T(8,128)(2,1)} %bitcast.50), calls=%async_computation.5 | async-start | bytes 6553600 | tf_op jit(solution)/shard_map/all_to_all | solution.py:77
  279.4 18.2 %all-to-all-start.1 = ((bf16[2,256,1024]{1,2,0:T(8,128)(2,1)}), bf16[2,256,1024]{1,2,0:T(8,128)(2,1)}, u32[]{:S(2)}, u32[]{:S(2)}) async-start(bf16[2,256,1024]{1,2,0:T(8,128)(2,1)} %copy.23), calls=%async_computation.1 | async-start | bytes 2097152 | tf_op jit(solution)/shard_map/all_to_all | solution.py:28
  297.6 13.9 %all-to-all-start.6 = ((bf16[2,256,800]{1,2,0:T(8,128)(2,1)}), bf16[2,256,800]{1,2,0:T(8,128)(2,1)S(1)}, u32[]{:S(2)}, u32[]{:S(2)}) async-start(bf16[2,256,800]{1,2,0:T(8,128)(2,1)} %bitcast.47), calls=%async_computation.6 | async-start | bytes 1638400 | tf_op jit(solution)/shard_map/all_to_all | solution.py:28
  311.5 0.9 copy-start.3
  312.4 101.1 %all-to-all-start.2 = ((bf16[8,96,2048]{2,1,0:T(8,128)(2,1)}), bf16[8,96,2048]{2,1,0:T(8,128)(2,1)S(1)}, u32[]{:S(2)}, u32[]{:S(2)}) async-start(bf16[8,96,2048]{2,1,0:T(8,128)(2,1)} %bitcast.52), calls=%async_computation.2 | async-start | bytes 6291456 | tf_op jit(solution)/shard_map/all_to_all | solution.py:53
  321.7 99.4 %copy-start.1 = (bf16[256,800]{0,1:T(8,128)(2,1)S(1)}, bf16[256,800]{0,1:T(8,128)(2,1)}, u32[]{:S(2)}) copy-start(bf16[256,800]{0,1:T(8,128)(2,1)} %param.6) | copy-start | bytes 1228804
  413.5 41.2 %all-to-all-start.7 = ((bf16[2,400,1024]{2,1,0:T(8,128)(2,1)}), bf16[2,400,1024]{2,1,0:T(8,128)(2,1)}, u32[]{:S(2)}, u32[]{:S(2)}) async-start(bf16[2,400,1024]{2,1,0:T(8,128)(2,1)} %bitcast.60), calls=%async_computation.8 | async-start | bytes 3276800 | tf_op jit(solution)/shard_map/all_to_all | solution.py:28
  420.2 0.9 copy-start
Sparse Core Ops, SparseCore 0:
  22.5 29.5 all-gather.2
  53.7 173.2 all-gather.4
  229.3 138.2 reduce-scatter.1
where the time goes:
time: 468 us; the launch traced here: 467 us
  waiting for transfers between devices  279 us (60%)
  blocking collectives  67.3 us (14%)
  starting transfers between devices  40.5 us (9%)
  local copies, waits for them, and re-layouts  29.5 us (6%)
  matrix products  23.1 us (5%)
  between operations  13.9 us (3%)
  other arithmetic  13.7 us (3%)
    all_to_all x2, waiting for transfers between devices, enc_exchange(): lax.all_to_all(x.reshape(senders, most_slots, out_cols), 'enc', split_axi...  227 us
    all_to_all x1, waiting for transfers between devices, body(): lax.all_to_all(pieces, features, split_axis=1, concat_axis=1, tiled=True)  27.1 us
    all_to_all x1, blocking collectives, near_exchange(): lax.all_to_all(x, 'enc', split, concat, axis_index_groups=near, tiled=True)  23 us
    all_to_all x4, starting transfers between devices, near_exchange(): lax.all_to_all(x, 'enc', split, concat, axis_index_groups=near, tiled=True)  22.3 us
    all_to_all x4, waiting for transfers between devices, near_exchange(): lax.all_to_all(x, 'enc', split, concat, axis_index_groups=near, tiled=True)  22.2 us
    psum x1, blocking collectives, body(): lax.psum((jnp.sum(owned_normalized_gradient * standardized_owned, 0), jnp...  20.9 us
    all_gather x1, blocking collectives, body(): lax.all_gather(patches, 'enc', axis=0, axis_index_groups=near, tiled=True)  15.1 us
    all_to_all x2, starting transfers between devices, enc_exchange(): lax.all_to_all(x.reshape(senders, most_slots, out_cols), 'enc', split_axi...  14.2 us
  transfers between devices with their start and end apart: 10, of which 7 were waited for; matrix products, arithmetic and copies ran while one was open for 13% of the time, Pallas kernels for 0%

commit v1 on v0

--- a/solution.py
+++ b/solution.py
@@ -74,7 +74,12 @@
     )
     group_count = width // owned_width
     pieces = partial_grad.astype(jnp.bfloat16).reshape(block * own_rows, group_count, owned_width)
-    columns = lax.all_to_all(pieces, features, split_axis=1, concat_axis=1, tiled=True)
+    columns = jnp.concatenate(
+        lax.all_to_all(
+            jnp.stack(jnp.split(pieces, lax.psum(1, features), 1), axis=0), features, 0, 0
+        ),
+        1,
+    )
     column_sum = jnp.sum(columns.astype(jnp.float32), 1).astype(jnp.bfloat16)
     shares = near_exchange(column_sum.reshape(block, own_rows, owned_width), 0, 0)
     owned_normalized_gradient = jnp.sum(shares.astype(jnp.float32), 0)

time: 468 us -> 468 us (level)
  waiting for transfers between devices: 279 us -> 274 us
  transfers between devices with their start and end apart: 10 -> 10, of which waited for: 7 -> 7; matrix products, arithmetic and copies ran while one was open for 13% -> 14% of each run, Pallas kernels for 0% -> 0%
where the time goes in v1:
time: 468 us; the launch traced here: 467 us
  waiting for transfers between devices  274 us (59%)
  blocking collectives  67.3 us (14%)
  starting transfers between devices  40.1 us (9%)
  local copies, waits for them, and re-layouts  30.7 us (7%)
  matrix products  24.8 us (5%)
  other arithmetic  15.6 us (3%)
  between operations  13.9 us (3%)
    all_to_all x2, waiting for transfers between devices, enc_exchange(): lax.all_to_all(x.reshape(senders, most_slots, out_cols), 'enc', split_axi...  223 us
    all_to_all x1, waiting for transfers between devices, body(): lax.all_to_all(jnp.stack(jnp.split(pieces, lax.psum(1, features), 1), axi...  27.1 us
    all_to_all x1, blocking collectives, near_exchange(): lax.all_to_all(x, 'enc', split, concat, axis_index_groups=near, tiled=True)  23 us
    all_to_all x4, starting transfers between devices, near_exchange(): lax.all_to_all(x, 'enc', split, concat, axis_index_groups=near, tiled=True)  22.3 us
    all_to_all x4, waiting for transfers between devices, near_exchange(): lax.all_to_all(x, 'enc', split, concat, axis_index_groups=near, tiled=True)  22.2 us
    psum x1, blocking collectives, body(): lax.psum((jnp.sum(owned_normalized_gradient * standardized_owned, 0), jnp...  20.9 us
    all_gather x1, blocking collectives, body(): lax.all_gather(patches, 'enc', axis=0, axis_index_groups=near, tiled=True)  15.1 us
    all_to_all x2, starting transfers between devices, enc_exchange(): lax.all_to_all(x.reshape(senders, most_slots, out_cols), 'enc', split_axi...  13.9 us
  transfers between devices with their start and end apart: 10, of which 7 were waited for; matrix products, arithmetic and copies ran while one was open for 14% of the time, Pallas kernels for 0%

profile of v1, /device:TPU:0, one launch (start us, length us, event | category | flops | bytes accessed | tf_op | source)
XLA Modules:
  0.0 466.7 jit_solution(10899816472604331814)
XLA Ops:
  7.2 15.1 %all_gather.9 = bf16[512,800]{0,1:T(8,128)(2,1)} all-gather(bf16[256,800]{0,1:T(8,128)(2,1)} %param.6), channel_id=1, replica_groups={{0,4},{8,12},{16,20},{24,28},{1,5},{9,13},{17,21},{25,29},{2,6},{10,14}..., dimensions={0}, use_global_device_ids=true | all-gather | bytes 1228800 | tf_op jit(solution)/shard_map/all_gather | solution.py:34
  22.4 1.6 copy.39
  24.0 23.0 %all_to_all.90 = bf16[400,2,1024]{2,0,1:T(8,128)(2,1)} all-to-all(bf16[400,2,1024]{2,0,1:T(8,128)(2,1)S(1)} %bitcast.62), channel_id=1, replica_groups={{0,4},{8,12},{16,20},{24,28},{1,5},{9,13},{17,21},{25,29},{2,6},{10,14}..., dimensions={1} | all-to-all | bytes 3276800 | tf_op jit(solution)/shard_map/all_to_all | solution.py:28
  47.0 4.9 %all-to-all-start.3 = ((bf16[8,96,2048]{2,1,0:T(8,128)(2,1)}), bf16[8,96,2048]{2,1,0:T(8,128)(2,1)S(1)}, u32[]{:S(2)}, u32[]{:S(2)}) async-start(bf16[8,96,2048]{2,1,0:T(8,128)(2,1)} %bitcast.66), calls=%async_computation.3 | async-start | bytes 6291456 | tf_op jit(solution)/shard_map/all_to_all | solution.py:53
  51.9 0.6 reduce-window.6
  52.5 0.2 slice_reduce_fusion
  52.8 0.1 fusion.8
  52.9 139.4 %all-to-all-done.3 = bf16[8,96,2048]{2,1,0:T(8,128)(2,1)S(1)} async-done(((bf16[8,96,2048]{2,1,0:T(8,128)(2,1)}), bf16[8,96,2048]{2,1,0:T(8,128)(2,1)S(1)}, u32[]{:S(2)}, u32[]{:S(2)}) %all-to-all-start.3) | async-done | bytes 3145760 | tf_op jit(solution)/shard_map/all_to_all | solution.py:53
  192.3 2.3 gather_fusion
  194.6 2.3 copy.40
  196.9 9.7 %all-to-all-start.4 = ((bf16[256,2,1024]{2,0,1:T(8,128)(2,1)}), bf16[256,2,1024]{2,0,1:T(8,128)(2,1)}, u32[]{:S(2)}, u32[]{:S(2)}) async-start(bf16[256,2,1024]{2,0,1:T(8,128)(2,1)} %bitcast.54), calls=%async_computation.4 | async-start | bytes 2097152 | tf_op jit(solution)/shard_map/all_to_all | solution.py:28
  206.6 3.0 convert_reduce_fusion
  209.6 7.6 %all-to-all-done.4 = bf16[256,2,1024]{2,0,1:T(8,128)(2,1)} async-done(((bf16[256,2,1024]{2,0,1:T(8,128)(2,1)}), bf16[256,2,1024]{2,0,1:T(8,128)(2,1)}, u32[]{:S(2)}, u32[]{:S(2)}) %all-to-all-start.4) | async-done | bytes 1048608 | tf_op jit(solution)/shard_map/all_to_all | solution.py:28
  217.2 7.5 %convolution_convert_fusion = bf16[3200,1024]{1,0:T(8,128)(2,1)} fusion(bf16[512,1024]{1,0:T(8,128)(2,1)} %bitcast.16, bf16[512,3200]{0,1:T(8,128)(2,1)S(1)} %copy-done.2, f32[3200]{0:T(1024)S(1)} %copy-done.8, f32[3200]{0:T(1024)S(1)} %copy-done.7, f32[512]{0:T(512)S(1)} %get-tuple-element.21, f32[512]{0:T(512)S(1)} %get-tuple-element.20), kind=kOutput, calls=%fused_computation.5 | convolution fusion | flops 3368550400 | bytes 10908672 | tf_op jit(solution)/shard_map/dot_general | solution.py:59
  224.8 2.2 all-gather.5.cloned.1.call-done
  227.0 8.6 %convolution_convert_fusion.1 = bf16[512,3200]{1,0:T(8,128)(2,1)} fusion(bf16[512,1024]{1,0:T(8,128)(2,1)} %bitcast.16, bf16[3200,1024]{1,0:T(8,128)(2,1)} %all-gather.5.cloned.1.call-done), kind=kOutput, calls=%fused_computation.11 | convolution fusion | flops 3357081600 | bytes 10878976 | tf_op jit(solution)/shard_map/dot_general | solution.py:72
  235.6 4.4 copy.29
  240.0 0.2 slice_bitcast_fusion.3
  240.3 1.9 pad_maximum_fusion
  242.2 3.9 all-to-all-start.5
  246.1 8.7 %convolution_convert_fusion.2 = bf16[512,1024]{1,0:T(8,128)(2,1)} fusion(bf16[3200,1024]{1,0:T(8,128)(2,1)} %all-gather.5.cloned.1.call-done, bf16[512,3200]{0,1:T(8,128)(2,1)} %all-gather.3.cloned.1.call-done, f32[3200]{0:T(1024)S(1)} %copy-done.8, f32[3200]{0:T(1024)S(1)} %copy-done.7, f32[512]{0:T(512)S(1)} %get-tuple-element.21, ...), kind=kOutput, calls=%fused_computation.19 | convolution fusion | flops 3365797888 | bytes 10908672 | tf_op jit(solution)/shard_map/dot_general | solution.py:68
  254.8 2.3 copy.26
  257.1 27.1 %all-to-all-done.5 = bf16[4,512,1,800]{1,3,2,0:T(8,128)(2,1)S(1)} async-done(((bf16[4,512,1,800]{1,3,2,0:T(8,128)(2,1)}), bf16[4,512,1,800]{1,3,2,0:T(8,128)(2,1)S(1)}, u32[]{:S(2)}, u32[]{:S(2)}) %all-to-all-start.5) | async-done | bytes 3276832 | tf_op jit(solution)/shard_map/all_to_all | solution.py:78
  284.2 4.4 all-to-all-start.1
  288.6 1.6 reduce_sum.90
  290.2 2.1 copy.41
  292.3 10.1 %all-to-all-done.1 = bf16[2,256,1024]{1,2,0:T(8,128)(2,1)} async-done(((bf16[2,256,1024]{1,2,0:T(8,128)(2,1)}), bf16[2,256,1024]{1,2,0:T(8,128)(2,1)}, u32[]{:S(2)}, u32[]{:S(2)}) %all-to-all-start.1) | async-done | bytes 1048608 | tf_op jit(solution)/shard_map/all_to_all | solution.py:28
  302.4 3.5 all-to-all-start.6
  305.9 1.5 copy.27
  307.4 4.3 scatter_custom_fusion
  311.7 4.6 all-to-all-done.6
  316.3 0.9 copy-done.3
  317.2 9.0 %all-to-all-start.2 = ((bf16[8,96,2048]{2,1,0:T(8,128)(2,1)}), bf16[8,96,2048]{2,1,0:T(8,128)(2,1)S(1)}, u32[]{:S(2)}, u32[]{:S(2)}) async-start(bf16[8,96,2048]{2,1,0:T(8,128)(2,1)} %bitcast.60), calls=%async_computation.2 | async-start | bytes 6291456 | tf_op jit(solution)/shard_map/all_to_all | solution.py:53
  326.2 1.4 dynamic_slice.8
  327.6 1.3 dynamic-slice.3
  328.9 1.3 dynamic-slice.4
  330.2 83.3 %all-to-all-done.2 = bf16[8,96,2048]{2,1,0:T(8,128)(2,1)S(1)} async-done(((bf16[8,96,2048]{2,1,0:T(8,128)(2,1)}), bf16[8,96,2048]{2,1,0:T(8,128)(2,1)S(1)}, u32[]{:S(2)}, u32[]{:S(2)}) %all-to-all-start.2) | async-done | bytes 3145760 | tf_op jit(solution)/shard_map/all_to_all | solution.py:53
  413.5 4.6 all-to-all-start.7
  418.2 2.0 convert_reduce_fusion.1
  420.2 0.9 copy-done
  421.1 1.7 multiply_reduce_fusion
  422.8 8.2 %all-reduce.1 = (f32[256]{0:T(256)}, f32[256]{0:T(256)}) all-reduce(f32[256]{0:T(256)} %get-tuple-element.8, f32[256]{0:T(256)} %get-tuple-element.9), channel_id=1, replica_groups=mesh['enc'=8,'section'=2,'llmdp'=2] {'section','llmdp'}, use_global_device_ids=true, to_apply=%region_11.12 | all-reduce | flops 512 | bytes 4096 | tf_op jit(solution)/shard_map/psum | solution.py:87
  431.0 20.9 %all-reduce = (f32[800]{0:T(1024)}, f32[800]{0:T(1024)}) all-reduce(f32[800]{0:T(1024)} %get-tuple-element.7, f32[800]{0:T(1024)} %get-tuple-element.10), channel_id=1, replica_groups=mesh['enc'=8,'section'=2,'llmdp'=2] {'enc'}, use_global_device_ids=true, to_apply=%region_14.15 | all-reduce | flops 1600 | bytes 12800 | tf_op jit(solution)/shard_map/psum | solution.py:104
  451.9 0.7 broadcast_multiply_fusion.1
  452.6 2.1 multiply_convert_fusion
  454.7 1.8 convert_bitcast_fusion
  456.6 1.9 copy.35
  458.5 1.7 copy.43
  (31 shorter events, 0.2 us)
Async XLA Ops:
  7.2 199.4 %all-gather.3.cloned.1.call-start = ((), (), s32[]{:S(2)}) async-start(), calls=%async_computation.9 | async-start | bytes 4096000 | tf_op jit(solution)/shard_map/all_gather | solution.py:35
  22.4 204.6 %all-gather.5.cloned.1.call-start = ((), (), s32[]{:S(2)}) async-start(), calls=%async_computation.10 | async-start | bytes 8192000 | tf_op jit(solution)/shard_map/all_gather | solution.py:33
  47.0 4.9 %copy-start.4 = (s32[256,1]{0,1:T(1,128)S(1)}, s32[256,1]{0,1:T(1,128)}, u32[]{:S(2)}) copy-start(s32[256,1]{0,1:T(1,128)} %param.10) | copy-start | bytes 3076
  47.0 145.3 %all-to-all-start.3 = ((bf16[8,96,2048]{2,1,0:T(8,128)(2,1)}), bf16[8,96,2048]{2,1,0:T(8,128)(2,1)S(1)}, u32[]{:S(2)}, u32[]{:S(2)}) async-start(bf16[8,96,2048]{2,1,0:T(8,128)(2,1)} %bitcast.66), calls=%async_computation.3 | async-start | bytes 6291456 | tf_op jit(solution)/shard_map/all_to_all | solution.py:53
  194.6 22.6 %copy-start.7 = (f32[3200]{0:T(1024)S(1)}, f32[3200]{0:T(1024)}, u32[]{:S(2)}) copy-start(f32[3200]{0:T(1024)} %param.7) | copy-start | bytes 38404
  194.6 22.6 %copy-start.8 = (f32[3200]{0:T(1024)S(1)}, f32[3200]{0:T(1024)}, u32[]{:S(2)}) copy-start(f32[3200]{0:T(1024)} %param.8) | copy-start | bytes 38404
  196.9 20.3 %all-to-all-start.4 = ((bf16[256,2,1024]{2,0,1:T(8,128)(2,1)}), bf16[256,2,1024]{2,0,1:T(8,128)(2,1)}, u32[]{:S(2)}, u32[]{:S(2)}) async-start(bf16[256,2,1024]{2,0,1:T(8,128)(2,1)} %bitcast.54), calls=%async_computation.4 | async-start | bytes 2097152 | tf_op jit(solution)/shard_map/all_to_all | solution.py:28
  206.6 206.9 %reduce-scatter.2.cloned.1.call-start = ((), (), s32[]{:S(2)}) async-start(), calls=%async_computation.11 | async-start | bytes 8192000 | tf_op jit(solution)/shard_map/reduce_scatter | solution.py:58
  206.6 10.6 %copy-start.2 = (bf16[512,3200]{0,1:T(8,128)(2,1)S(1)}, bf16[512,3200]{0,1:T(8,128)(2,1)}, u32[]{:S(2)}) copy-start(bf16[512,3200]{0,1:T(8,128)(2,1)} %all-gather.3.cloned.1.call-done) | copy-start | bytes 9830404
  209.6 36.5 %copy-start.5 = (f32[512]{0:T(512)}, f32[512]{0:T(512)S(1)}, u32[]{:S(2)}) copy-start(f32[512]{0:T(512)S(1)} %get-tuple-element.21) | copy-start | bytes 6148
  209.6 36.5 %copy-start.6 = (f32[512]{0:T(512)}, f32[512]{0:T(512)S(1)}, u32[]{:S(2)}) copy-start(f32[512]{0:T(512)S(1)} %get-tuple-element.20) | copy-start | bytes 6148
  242.2 42.0 %all-to-all-start.5 = ((bf16[4,512,1,800]{1,3,2,0:T(8,128)(2,1)}), bf16[4,512,1,800]{1,3,2,0:T(8,128)(2,1)S(1)}, u32[]{:S(2)}, u32[]{:S(2)}) async-start(bf16[4,512,1,800]{1,3,2,0:T(8,128)(2,1)} %pad_maximum_fusion), calls=%async_computation.5 | async-start | bytes 6553600 | tf_op jit(solution)/shard_map/all_to_all | solution.py:78
  284.2 18.2 %all-to-all-start.1 = ((bf16[2,256,1024]{1,2,0:T(8,128)(2,1)}), bf16[2,256,1024]{1,2,0:T(8,128)(2,1)}, u32[]{:S(2)}, u32[]{:S(2)}) async-start(bf16[2,256,1024]{1,2,0:T(8,128)(2,1)} %copy.26), calls=%async_computation.1 | async-start | bytes 2097152 | tf_op jit(solution)/shard_map/all_to_all | solution.py:28
  302.4 13.9 %all-to-all-start.6 = ((bf16[2,256,800]{1,2,0:T(8,128)(2,1)}), bf16[2,256,800]{1,2,0:T(8,128)(2,1)S(1)}, u32[]{:S(2)}, u32[]{:S(2)}) async-start(bf16[2,256,800]{1,2,0:T(8,128)(2,1)} %bitcast.55), calls=%async_computation.6 | async-start | bytes 1638400 | tf_op jit(solution)/shard_map/all_to_all | solution.py:28
  316.3 0.9 copy-start.3
  317.2 96.3 %all-to-all-start.2 = ((bf16[8,96,2048]{2,1,0:T(8,128)(2,1)}), bf16[8,96,2048]{2,1,0:T(8,128)(2,1)S(1)}, u32[]{:S(2)}, u32[]{:S(2)}) async-start(bf16[8,96,2048]{2,1,0:T(8,128)(2,1)} %bitcast.60), calls=%async_computation.2 | async-start | bytes 6291456 | tf_op jit(solution)/shard_map/all_to_all | solution.py:53
  326.2 94.9 %copy-start.1 = (bf16[256,800]{0,1:T(8,128)(2,1)S(1)}, bf16[256,800]{0,1:T(8,128)(2,1)}, u32[]{:S(2)}) copy-start(bf16[256,800]{0,1:T(8,128)(2,1)} %param.6) | copy-start | bytes 1228804
  413.5 41.2 %all-to-all-start.7 = ((bf16[2,400,1024]{2,1,0:T(8,128)(2,1)}), bf16[2,400,1024]{2,1,0:T(8,128)(2,1)}, u32[]{:S(2)}, u32[]{:S(2)}) async-start(bf16[2,400,1024]{2,1,0:T(8,128)(2,1)} %bitcast.68), calls=%async_computation.8 | async-start | bytes 3276800 | tf_op jit(solution)/shard_map/all_to_all | solution.py:28
  420.2 0.9 copy-start
Sparse Core Ops, SparseCore 0:
  22.5 29.5 all-gather.2
  53.7 173.2 all-gather.4
  229.3 133.9 reduce-scatter.1
